TPU v7x, 256 devices: a 8x8x2 block of a 8x8x16 slice. The times are simulated.
256 devices in a mesh: groups: 2 (over z), ep: 64 (over y, x), tp: 2 (over core).
Axes of the slice: x: 8, y: 8, z: 2, core: 2. Of those that a mesh axis runs over, the one named last changes fastest.
The devices are a block of a 8x8x16 slice.
Arguments:
- hidden: bfloat16 [2048, 3584], P(('groups', 'ep'), 'tp'), parts along dimension 0, may hold values from -6 to 6
- routes: int32 [2048, 8], P(('groups', 'ep')), parts along dimension 0, may hold values from 0 to 63, as said below
- router_weight: bfloat16 [3584, 64], P('tp'), may hold values from -0.1875 to 0.1875
- gate_weight: bfloat16 [64, 3584, 1024], P('ep', None, 'tp'), may hold values from -0.09375 to 0.09375
- up_weight: bfloat16 [64, 3584, 1024], P('ep', None, 'tp'), may hold values from -0.09375 to 0.09375
- down_weight: bfloat16 [64, 1024, 3584], P('ep', 'tp'), may hold values from -0.1875 to 0.1875
- q_latent: bfloat16 [512, 64, 512], P(('groups', 'ep'), 'tp'), parts along dimension 0, may hold values from -48 to 48
- q_rope: bfloat16 [512, 64, 64], P(('groups', 'ep'), 'tp'), parts along dimension 0, may hold values from -48 to 48
- cache_latent: bfloat16 [512, 256, 512], P(('groups', 'ep')), parts along dimension 0, may hold values from -4 to 4
- cache_rope: bfloat16 [512, 64, 256], P(('groups', 'ep')), parts along dimension 0, may hold values from -4 to 4
- lengths: int32 [512], P(('groups', 'ep')), parts along dimension 0, may hold values from 16 to 256, as said below
Outputs:
- moe_out: bfloat16 [2048, 3584], P(('groups', 'ep'), 'tp'), parts along dimension 0
- attn_latent: bfloat16 [512, 64, 512], P(('groups', 'ep'), 'tp'), parts along dimension 0
There are 2 independent parts, one for each index of `groups`. A program takes and returns all parts, laid end to end along the dimension named above; an argument that names none is the same for every part. Nothing has to cross between parts.
Inputs may be any that keep to these rules, and one draw needn't show every extreme that they name: `routes`: each row names 8 different experts; in each aligned block of 16 rows (the rows of one index of ep) no expert is named more than 8 times, and one expert, the same in every block, is named exactly 8 times in each block. `lengths`: one sequence has 256 live positions and one has 16.
All inputs are finite; a program needn't handle non-finite values.
Results may differ from a plain program's by a relative error of at most 0.0085.
Values may be sent and summed in bfloat16 or wider, within the bound.
No kernel may reach another device: no remote copies, remote signals or barrier semaphores. Data moves between devices by JAX's collectives and lax.ppermute only.
A program may use at most 128 MiB of HBM per device.

v0:
```python
import jax
import jax.numpy as jnp
from jax import lax
from jax.sharding import PartitionSpec as P

softmax_scale = 192.0 ** (-0.5)
routed_scale = 2.5


def gathered_total(value, axis):
    tiles = lax.all_gather(value, axis)
    return tiles.sum(axis=0)


def in_blocks(value, dim, devices):
    lengths = value.shape
    tiles = value.reshape(*lengths[:dim], devices, lengths[dim] // devices, *lengths[dim + 1 :])
    return jnp.moveaxis(tiles, dim, 0)


def sum_at_owner(value, axis, dim):
    devices = lax.axis_size(axis)
    tiles = lax.all_to_all(in_blocks(value, dim, devices), axis, 0, 0, tiled=True)
    return jnp.sum(tiles, axis=0)


def local(
    hidden,
    routes,
    router_weight,
    gate_weight,
    up_weight,
    down_weight,
    q_latent,
    q_rope,
    cache_latent,
    cache_rope,
    lengths,
):
    token_count, top_count = routes.shape
    expert_count = lax.axis_size("ep")
    capacity = min(token_count, 4 * token_count * top_count // expert_count)
    partial_logits = jnp.dot(hidden, router_weight, preferred_element_type=jnp.float32)
    logits = gathered_total(partial_logits, "tp")
    affinity = jax.nn.sigmoid(logits)
    expert_iota = jnp.arange(expert_count, dtype=jnp.int32)
    chosen_mask = routes[:, :, None] == expert_iota[None, None, :]
    chosen = jnp.sum(jnp.where(chosen_mask, affinity[:, None, :], 0.0), axis=2)
    gates = routed_scale * chosen / jnp.sum(chosen, axis=1, keepdims=True)
    flat_mask = chosen_mask.reshape(token_count * top_count, expert_count).astype(jnp.int32)
    earlier = jnp.cumsum(flat_mask, axis=0) - flat_mask
    within = jnp.sum(flat_mask * earlier, axis=1).reshape(token_count, top_count)
    slot_index = routes * capacity + within
    slot_iota = jnp.arange(expert_count * capacity, dtype=jnp.int32)
    placing = jnp.sum(
        (slot_index[None, :, :] == slot_iota[:, None, None]).astype(jnp.int32), axis=2
    )
    placing = placing.astype(jnp.bfloat16)
    outgoing = jnp.dot(placing, hidden, preferred_element_type=jnp.float32).astype(jnp.bfloat16)
    outgoing = outgoing.reshape(expert_count, capacity, hidden.shape[1])
    received = lax.all_to_all(outgoing, "ep", split_axis=0, concat_axis=0, tiled=True)
    received = lax.all_gather(received, "tp", axis=2, tiled=True)
    source_count, slot_count, feature_count = received.shape
    flat_rows = received.reshape(source_count * slot_count, feature_count)
    gate_part = jnp.dot(flat_rows, gate_weight[0], preferred_element_type=jnp.float32)
    up_part = jnp.dot(flat_rows, up_weight[0], preferred_element_type=jnp.float32)
    active = (jax.nn.silu(gate_part) * up_part).astype(jnp.bfloat16)
    partial_out = jnp.dot(active, down_weight[0], preferred_element_type=jnp.float32)
    summed = sum_at_owner(partial_out, "tp", 1).astype(jnp.bfloat16)
    summed = summed.reshape(source_count, slot_count, summed.shape[1])
    returned = lax.all_to_all(summed, "ep", split_axis=0, concat_axis=0, tiled=True)
    scores = jnp.einsum("bhl,bjl->bhj", q_latent, cache_latent, preferred_element_type=jnp.float32)
    scores = scores + jnp.einsum(
        "bhr,brj->bhj", q_rope, cache_rope, preferred_element_type=jnp.float32
    )
    scores = scores * softmax_scale
    position = jnp.arange(cache_latent.shape[1], dtype=jnp.int32)
    live = position[None, None, :] < lengths[:, None, None]
    scores = jnp.where(live, scores, -jnp.inf)
    highest = jnp.max(scores, axis=2, keepdims=True)
    expo = jnp.where(live, jnp.exp(scores - highest), 0.0)
    attn_probs = (expo / jnp.sum(expo, axis=2, keepdims=True)).astype(jnp.bfloat16)
    attn_latent = jnp.einsum(
        "bhj,bjl->bhl", attn_probs, cache_latent, preferred_element_type=jnp.float32
    )
    attn_latent = attn_latent.astype(jnp.bfloat16)
    returned_flat = returned.reshape(expert_count * capacity, returned.shape[2])
    picked = jnp.take(returned_flat, slot_index.reshape(-1), axis=0).reshape(
        token_count, top_count, returned.shape[2]
    )
    moe_out = jnp.sum(gates[:, :, None] * picked.astype(jnp.float32), axis=1).astype(jnp.bfloat16)
    return (moe_out, attn_latent)


def solution(mesh):
    return jax.shard_map(
        local,
        mesh=mesh,
        in_specs=(
            P(("groups", "ep"), "tp"),
            P(("groups", "ep"), None),
            P("tp", None),
            P("ep", None, "tp"),
            P("ep", None, "tp"),
            P("ep", "tp", None),
            P(("groups", "ep"), "tp", None),
            P(("groups", "ep"), "tp", None),
            P(("groups", "ep"), None, None),
            P(("groups", "ep"), None, None),
            P(("groups", "ep")),
        ),
        out_specs=(P(("groups", "ep"), "tp"), P(("groups", "ep"), "tp", None)),
        check_vma=False,
    )
```

profile of v0, /device:TPU:514, one launch (start us, length us, event | category | flops | bytes accessed | tf_op | source)
XLA Modules:
  0.0 199.2 jit_solution(17828745028653575509)
XLA Ops:
  7.3 0.8 copy.21
  8.3 0.2 reduce_window_sum.11
  8.5 0.2 select_reduce_fusion.2
  8.7 0.1 convert_reduce_fusion
  8.9 1.5 fusion.7
  10.4 66.5 %all_to_all.15 = bf16[64,8,1792]{2,1,0:T(8,128)(2,1)} all-to-all(bf16[64,8,1792]{2,1,0:T(8,128)(2,1)S(1)} %fusion.7), channel_id=1, replica_groups=mesh['groups'=2,'ep'=64,'tp'=2] {'ep'}, dimensions={0} | all-to-all | bytes 3670016 | tf_op jit(solution)/shard_map/all_to_all | solution.py:61
  77.0 6.0 %copy.25 = bf16[3584,512]{1,0:T(8,128)(2,1)} copy(bf16[3584,512]{0,1:T(8,128)(2,1)} %bitcast.59) | data formatting | bytes 7340032 | tf_op jit(solution)/shard_map/dot_general | solution.py:68
  82.9 20.7 %all-gather.3.cloned.1.call-done = bf16[64,8,3584]{2,1,0:T(8,128)(2,1)} async-done(((bf16[64,8,1792]{2,1,0:T(8,128)(2,1)}), bf16[64,8,3584]{2,1,0:T(8,128)(2,1)}) %all-gather.3.cloned.1.call-update) | async-done | bytes 3670032 | tf_op jit(solution)/shard_map/all_gather | solution.py:62
  103.6 5.3 %fusion.3 = f32[512,512]{1,0:T(8,128)S(1)} fusion(bf16[1,3584,512]{2,1,0:T(8,128)(2,1)} %param.14, bf16[64,8,3584]{2,1,0:T(8,128)(2,1)} %all-gather.3.cloned.1.call-done), kind=kOutput, calls=%fused_computation.5 | convolution fusion | flops 1879048192 | bytes 8388608 | tf_op jit(solution)/shard_map/dot_general | solution.py:65
  109.0 2.1 %fusion.18 = bf16[512,512,1]{1,0,2:T(8,128)(2,1)S(1)} fusion(bf16[1,3584,512]{2,1,0:T(8,128)(2,1)S(1)} %copy-done.7, bf16[64,8,3584]{2,1,0:T(8,128)(2,1)S(1)} %copy-done.8, f32[512,512]{1,0:T(8,128)S(1)} %fusion.3), kind=kOutput, calls=%fused_computation.14 | convolution fusion | flops 1880621056 | bytes 8912896 | tf_op jit(solution)/shard_map/dot_general | solution.py:66
  111.2 2.1 %convolution_bitcast_fusion = f32[2,512,1792]{2,1,0:T(8,128)S(1)} fusion(bf16[512,512,1]{1,0,2:T(8,128)(2,1)S(1)} %fusion.18, bf16[2,1792,512]{2,1,0:T(8,128)(2,1)S(1)} %bitcast.57), kind=kOutput, calls=%fused_computation.2 | convolution fusion | flops 1879048192 | bytes 11534336 | tf_op jit(solution)/shard_map/dot_general | solution.py:68
  113.3 10.9 %all_to_all.16 = f32[2,512,1792]{2,1,0:T(8,128)} all-to-all(f32[2,512,1792]{2,1,0:T(8,128)S(1)} %convolution_bitcast_fusion), channel_id=1, replica_groups=mesh['groups'=2,'ep'=64,'tp'=2] {'tp'}, dimensions={0} | all-to-all | bytes 14680064 | tf_op jit(solution)/shard_map/all_to_all | solution.py:23
  124.2 5.5 %reduce_sum.77 = bf16[512,1792]{1,0:T(8,128)(2,1)} reduce(f32[2,512,1792]{2,1,0:T(8,128)} %all_to_all.16, f32[]{:T(128)} %constant.13.clone.1), dimensions={0}, to_apply=%region_6.7 | reduce | flops 917504 | bytes 9175044 | tf_op jit(solution)/shard_map/reduce_sum | solution.py:24
  129.7 13.8 %all-to-all-start.2 = ((bf16[64,8,1792]{2,1,0:T(8,128)(2,1)}), bf16[64,8,1792]{2,1,0:T(8,128)(2,1)S(1)}, u32[]{:S(2)}, u32[]{:S(2)}) async-start(bf16[64,8,1792]{2,1,0:T(8,128)(2,1)} %bitcast.58), calls=%async_computation.2 | async-start | bytes 3670016 | tf_op jit(solution)/shard_map/all_to_all | solution.py:71
  143.6 0.1 fusion.35
  143.8 1.9 all-gather
  145.7 0.3 select_reduce_fusion
  146.1 0.4 fusion.36
  146.5 0.1 fusion.27
  146.7 0.2 fusion.34
  146.9 1.0 convolution_convert_fusion.1
  147.9 42.2 %all-to-all-done.2 = bf16[64,8,1792]{2,1,0:T(8,128)(2,1)S(1)} async-done(((bf16[64,8,1792]{2,1,0:T(8,128)(2,1)}), bf16[64,8,1792]{2,1,0:T(8,128)(2,1)S(1)}, u32[]{:S(2)}, u32[]{:S(2)}) %all-to-all-start.2) | async-done | bytes 1835040 | tf_op jit(solution)/shard_map/all_to_all | solution.py:71
  190.1 0.9 gather_fusion
  191.0 1.3 multiply_reduce_fusion
  (33 shorter events, 0.7 us)
Async XLA Ops:
  7.2 138.9 %copy-start = (bf16[4,256,512]{2,1,0:T(8,128)(2,1)S(1)}, bf16[4,256,512]{2,1,0:T(8,128)(2,1)}, u32[]{:S(2)}) copy-start(bf16[4,256,512]{2,1,0:T(8,128)(2,1)} %param.19) | copy-start | bytes 3145732
  7.2 96.4 %all-gather.3.cloned.1.call-start = ((), (), s32[]{:S(2)}) async-start(), calls=%async_computation.3 | async-start | bytes 5505024 | tf_op jit(solution)/shard_map/all_gather | solution.py:62
  103.6 5.4 %copy-start.7 = (bf16[1,3584,512]{2,1,0:T(8,128)(2,1)S(1)}, bf16[1,3584,512]{2,1,0:T(8,128)(2,1)}, u32[]{:S(2)}) copy-start(bf16[1,3584,512]{2,1,0:T(8,128)(2,1)} %param.15) | copy-start | bytes 11010052
  103.6 5.4 %copy-start.8 = (bf16[64,8,3584]{2,1,0:T(8,128)(2,1)S(1)}, bf16[64,8,3584]{2,1,0:T(8,128)(2,1)}, u32[]{:S(2)}) copy-start(bf16[64,8,3584]{2,1,0:T(8,128)(2,1)} %all-gather.3.cloned.1.call-done) | copy-start | bytes 11010052
  109.0 2.2 %copy-start.1 = (bf16[3584,512]{1,0:T(8,128)(2,1)S(1)}, bf16[3584,512]{1,0:T(8,128)(2,1)}, u32[]{:S(2)}) copy-start(bf16[3584,512]{1,0:T(8,128)(2,1)} %copy.25) | copy-start | bytes 11010052
  129.6 14.0 %copy-start.2 = (bf16[1792,64]{0,1:T(8,128)(2,1)S(1)}, bf16[1792,64]{0,1:T(8,128)(2,1)}, u32[]{:S(2)}) copy-start(bf16[1792,64]{0,1:T(8,128)(2,1)} %param.13) | copy-start | bytes 688132
  129.6 14.0 %copy-start.3 = (bf16[16,1792]{1,0:T(8,128)(2,1)S(1)}, bf16[16,1792]{1,0:T(8,128)(2,1)}, u32[]{:S(2)}) copy-start(bf16[16,1792]{1,0:T(8,128)(2,1)} %param.11) | copy-start | bytes 172036
  129.6 16.4 %copy-start.9 = (s32[4]{0:T(128)S(1)}, s32[4]{0:T(128)}, u32[]{:S(2)}) copy-start(s32[4]{0:T(128)} %param.21) | copy-start | bytes 52
  129.6 16.4 %copy-start.4 = (bf16[4,32,512]{2,1,0:T(8,128)(2,1)S(1)}, bf16[4,32,512]{2,1,0:T(8,128)(2,1)}, u32[]{:S(2)}) copy-start(bf16[4,32,512]{2,1,0:T(8,128)(2,1)} %param.17) | copy-start | bytes 393220
  129.6 16.8 %copy-start.5 = (bf16[4,64,256]{2,1,0:T(8,128)(2,1)S(1)}, bf16[4,64,256]{2,1,0:T(8,128)(2,1)}, u32[]{:S(2)}) copy-start(bf16[4,64,256]{2,1,0:T(8,128)(2,1)} %param.20) | copy-start | bytes 393220
  129.6 16.9 %copy-start.6 = (bf16[4,32,64]{2,1,0:T(8,128)(2,1)S(1)}, bf16[4,32,64]{2,1,0:T(8,128)(2,1)}, u32[]{:S(2)}) copy-start(bf16[4,32,64]{2,1,0:T(8,128)(2,1)} %param.18) | copy-start | bytes 49156
  129.7 60.4 %all-to-all-start.2 = ((bf16[64,8,1792]{2,1,0:T(8,128)(2,1)}), bf16[64,8,1792]{2,1,0:T(8,128)(2,1)S(1)}, u32[]{:S(2)}, u32[]{:S(2)}) async-start(bf16[64,8,1792]{2,1,0:T(8,128)(2,1)} %bitcast.58), calls=%async_computation.2 | async-start | bytes 3670016 | tf_op jit(solution)/shard_map/all_to_all | solution.py:71
Sparse Core Ops, SparseCore 0:
  77.1 26.4 all-gather.2
where the time goes:
time: 200 us; the launch traced here: 199 us
  blocking collectives  79.3 us (40%)
  waiting for transfers between devices  62.9 us (31%)
  between operations  14.2 us (7%)
  starting transfers between devices  13.9 us (7%)
  matrix products  12.8 us (6%)
  local copies, waits for them, and re-layouts  8.03 us (4%)
  other arithmetic  8.02 us (4%)
    all_to_all x1, blocking collectives, local(): lax.all_to_all(outgoing, 'ep', split_axis=0, concat_axis=0, tiled=True)  66.5 us
    all_to_all x1, waiting for transfers between devices, local(): lax.all_to_all(summed, 'ep', split_axis=0, concat_axis=0, tiled=True)  42.2 us
    all_gather x1, waiting for transfers between devices, local(): received = lax.all_gather(received, 'tp', axis=2, tiled=True)  20.7 us
    all_to_all x1, starting transfers between devices, local(): lax.all_to_all(summed, 'ep', split_axis=0, concat_axis=0, tiled=True)  13.8 us
    all_to_all x1, blocking collectives, sum_at_owner(): lax.all_to_all(in_blocks(value, dim, devices), axis, 0, 0, tiled=True)  10.9 us
    dot_general x1, local copies, waits for them, and re-layouts, local(): jnp.dot(active, down_weight[0], preferred_element_type=jnp.float32)  5.96 us
    reduce_sum x1, other arithmetic, sum_at_owner(): return jnp.sum(tiles, axis=0)  5.46 us
    dot_general x1, matrix products, local(): jnp.dot(flat_rows, gate_weight[0], preferred_element_type=jnp.float32)  5.34 us
  transfers between devices with their start and end apart: 2, of which 2 were waited for; matrix products, arithmetic and copies ran while one was open for 4% of the time, Pallas kernels for 0%

commit v1 on v0

--- a/solution.py
+++ b/solution.py
@@ -12,16 +12,18 @@
     return tiles.sum(axis=0)
 
 
-def in_blocks(value, dim, devices):
-    lengths = value.shape
-    tiles = value.reshape(*lengths[:dim], devices, lengths[dim] // devices, *lengths[dim + 1 :])
-    return jnp.moveaxis(tiles, dim, 0)
+def swapped(value, axis):
+    return lax.ppermute(value, axis, [(0, 1), (1, 0)])
 
 
-def sum_at_owner(value, axis, dim):
-    devices = lax.axis_size(axis)
-    tiles = lax.all_to_all(in_blocks(value, dim, devices), axis, 0, 0, tiled=True)
-    return jnp.sum(tiles, axis=0)
+def half_dot(rows, weight, start):
+    part = lax.dynamic_slice_in_dim(weight, start, rows.shape[1], 0)
+    return jnp.dot(rows, part, preferred_element_type=jnp.float32)
+
+
+def half_out(rows, weight, start, width):
+    part = lax.dynamic_slice_in_dim(weight, start, width, 1)
+    return jnp.dot(rows, part, preferred_element_type=jnp.float32)
 
 
 def local(
@@ -59,15 +61,18 @@
     outgoing = jnp.dot(placing, hidden, preferred_element_type=jnp.float32).astype(jnp.bfloat16)
     outgoing = outgoing.reshape(expert_count, capacity, hidden.shape[1])
     received = lax.all_to_all(outgoing, "ep", split_axis=0, concat_axis=0, tiled=True)
-    received = lax.all_gather(received, "tp", axis=2, tiled=True)
-    source_count, slot_count, feature_count = received.shape
-    flat_rows = received.reshape(source_count * slot_count, feature_count)
-    gate_part = jnp.dot(flat_rows, gate_weight[0], preferred_element_type=jnp.float32)
-    up_part = jnp.dot(flat_rows, up_weight[0], preferred_element_type=jnp.float32)
+    source_count, slot_count, half = received.shape
+    own_rows = received.reshape(source_count * slot_count, half)
+    other_rows = swapped(own_rows, "tp")
+    mine = lax.axis_index("tp") * half
+    theirs = half - mine
+    gate_part = half_dot(own_rows, gate_weight[0], mine) + half_dot(other_rows, gate_weight[0], theirs)
+    up_part = half_dot(own_rows, up_weight[0], mine) + half_dot(other_rows, up_weight[0], theirs)
     active = (jax.nn.silu(gate_part) * up_part).astype(jnp.bfloat16)
-    partial_out = jnp.dot(active, down_weight[0], preferred_element_type=jnp.float32)
-    summed = sum_at_owner(partial_out, "tp", 1).astype(jnp.bfloat16)
-    summed = summed.reshape(source_count, slot_count, summed.shape[1])
+    sent_part = half_out(active, down_weight[0], theirs, half).astype(jnp.bfloat16)
+    kept_part = half_out(active, down_weight[0], mine, half)
+    summed = (kept_part + swapped(sent_part, "tp").astype(jnp.float32)).astype(jnp.bfloat16)
+    summed = summed.reshape(source_count, slot_count, half)
     returned = lax.all_to_all(summed, "ep", split_axis=0, concat_axis=0, tiled=True)
     scores = jnp.einsum("bhl,bjl->bhj", q_latent, cache_latent, preferred_element_type=jnp.float32)
     scores = scores + jnp.einsum(

time: 200 us -> 147 us (0.73)
  waiting for transfers between devices: 62.9 us -> 45.7 us
  between operations: 14.2 us -> 0.84 us
  blocking collectives: 79.3 us -> 67.9 us
  other arithmetic: 8.02 us -> 2.56 us
  local copies, waits for them, and re-layouts: 8.03 us -> 2.99 us
  starting transfers between devices: 13.9 us -> 9.69 us
  matrix products: 12.8 us -> 16.1 us
    all_gather x1 -> x0, waiting for transfers between devices: 20.7 us -> none  [local(): received = lax.all_gather(received, 'tp', axis=2, tiled=True)]
    all_to_all x1 -> x0, blocking collectives: 10.9 us -> none  [sum_at_owner(): lax.all_to_all(in_blocks(value, dim, devices), axis, 0, 0, tiled=True)]
    dot_general x1 -> x0, local copies, waits for them, and re-layouts: 5.96 us -> none  [local(): jnp.dot(active, down_weight[0], preferred_element_type=jnp.float32)]
    reduce_sum x1 -> x0, other arithmetic: 5.46 us -> none  [sum_at_owner(): return jnp.sum(tiles, axis=0)]
    all_to_all x1, starting transfers between devices: 13.8 us -> 9.06 us  [local(): lax.all_to_all(summed, 'ep', split_axis=0, concat_axis=0, tiled=True)]
    ppermute x0 -> x2, waiting for transfers between devices: none -> 3.42 us  [swapped(): return lax.ppermute(value, axis, [(0, 1), (1, 0)])]
    dot_general x3 -> x6, matrix products: 9.59 us -> 12.9 us  [the longest x4 9.38 us: half_dot(): return jnp.dot(rows, part, preferred_element_type=jnp.float32)]
  transfers between devices with their start and end apart: 2 -> 3, of which waited for: 2 -> 2; matrix products, arithmetic and copies ran while one was open for 4% -> 4% of each run, Pallas kernels for 0% -> 0%
where the time goes in v1:
time: 147 us; the launch traced here: 146 us
  blocking collectives  67.9 us (46%)
  waiting for transfers between devices  45.7 us (31%)
  matrix products  16.1 us (11%)
  starting transfers between devices  9.69 us (7%)
  local copies, waits for them, and re-layouts  2.99 us (2%)
  other arithmetic  2.56 us (2%)
    all_to_all x1, blocking collectives, local(): lax.all_to_all(outgoing, 'ep', split_axis=0, concat_axis=0, tiled=True)  66 us
    all_to_all x1, waiting for transfers between devices, local(): lax.all_to_all(summed, 'ep', split_axis=0, concat_axis=0, tiled=True)  42.3 us
    dot_general x4, matrix products, half_dot(): return jnp.dot(rows, part, preferred_element_type=jnp.float32)  9.38 us
    all_to_all x1, starting transfers between devices, local(): lax.all_to_all(summed, 'ep', split_axis=0, concat_axis=0, tiled=True)  9.06 us
    dot_general x2, matrix products, half_out(): return jnp.dot(rows, part, preferred_element_type=jnp.float32)  3.53 us
    ppermute x2, waiting for transfers between devices, swapped(): return lax.ppermute(value, axis, [(0, 1), (1, 0)])  3.42 us
  transfers between devices with their start and end apart: 3, of which 2 were waited for; matrix products, arithmetic and copies ran while one was open for 4% of the time, Pallas kernels for 0%

profile of v1, /device:TPU:514, one launch (start us, length us, event | category | flops | bytes accessed | tf_op | source)
XLA Modules:
  0.0 145.7 jit_solution(13831287852706244738)
XLA Ops:
  0.6 0.8 copy.19
  1.7 0.2 reduce_window_sum.11
  1.8 0.2 select_reduce_fusion.2
  2.3 1.5 %fusion.1 = bf16[64,8,1792]{2,1,0:T(8,128)(2,1)S(1)} fusion(bf16[16,1792]{1,0:T(8,128)(2,1)} %param.11, s32[512,16]{0,1:T(8,128)S(1)} %convert_reduce_fusion), kind=kOutput, calls=%fused_computation.5 | convolution fusion | flops 30285824 | bytes 1925120 | tf_op jit(solution)/shard_map/dot_general | solution.py:61
  3.8 66.0 %all_to_all.10 = bf16[64,8,1792]{2,1,0:T(8,128)(2,1)S(1)} all-to-all(bf16[64,8,1792]{2,1,0:T(8,128)(2,1)S(1)} %fusion.1), channel_id=1, replica_groups=mesh['groups'=2,'ep'=64,'tp'=2] {'ep'}, dimensions={0} | all-to-all | bytes 3670016 | tf_op jit(solution)/shard_map/all_to_all | solution.py:63
  69.8 2.8 %fusion.14 = f32[512,512]{1,0:T(8,128)S(1)} fusion(bf16[1,3584,512]{2,1,0:T(8,128)(2,1)} %param.14, s32[]{:T(128)S(6)} %select_n.45, bf16[64,8,1792]{2,1,0:T(8,128)(2,1)S(1)} %all_to_all.10), kind=kOutput, calls=%fused_computation.16 | convolution fusion | flops 939524096 | bytes 4718596 | tf_op jit(solution)/shard_map/dot_general | solution.py:21
  72.6 1.1 fusion.10
  73.7 0.9 copy-done.6
  74.6 2.6 %fusion.22 = f32[512,512]{1,0:T(8,128)S(1)} fusion(f32[512,512]{1,0:T(8,128)S(1)} %fusion.14, bf16[512,1792]{1,0:T(8,128)(2,1)} %collective-permute-done, bf16[1,3584,512]{2,1,0:T(8,128)(2,1)S(1)} %copy-done.6, s32[]{:T(128)S(6)} %select_n.46), kind=kOutput, calls=%fused_computation.24 | convolution fusion | flops 939786240 | bytes 5767172 | tf_op jit(solution)/shard_map/dot_general | solution.py:21
  77.2 2.9 %multiply_convert_fusion = bf16[512,512]{1,0:T(8,128)(2,1)S(1)} fusion(f32[512,512]{1,0:T(8,128)S(1)} %fusion.22, f32[512,512]{1,0:T(8,128)S(1)} %fusion.10, bf16[512,1792]{1,0:T(8,128)(2,1)} %collective-permute-done, bf16[1,3584,512]{2,1,0:T(8,128)(2,1)S(1)} %copy-done.7, s32[]{:T(128)S(6)} %select_n.46), kind=kOutput, calls=%fused_computation.33 | convolution fusion | flops 941359104 | bytes 6291460 | tf_op jit(solution)/shard_map/dot_general | solution.py:21
  80.2 1.1 convolution_convert_fusion
  81.3 0.6 collective-permute-start.1
  81.9 3.4 %collective-permute-done.1 = bf16[512,1792]{1,0:T(8,128)(2,1)S(1)} collective-permute-done((bf16[512,1792]{1,0:T(8,128)(2,1)S(1)}, bf16[512,1792]{1,0:T(8,128)(2,1)S(1)}, u32[]{:S(2)}, u32[]{:S(2)}) %collective-permute-start.1) | collective-permute-done | bytes 1835040 | tf_op jit(solution)/shard_map/ppermute | solution.py:16
  85.3 2.4 %fusion.2 = bf16[64,8,1792]{2,1,0:T(8,128)(2,1)} fusion(bf16[512,1792]{1,0:T(8,128)(2,1)S(1)} %collective-permute-done.1, bf16[512,512]{1,0:T(8,128)(2,1)S(1)} %multiply_convert_fusion, bf16[1,512,3584]{2,1,0:T(8,128)(2,1)S(1)} %copy-done.8, s32[]{:T(128)S(6)} %select_n.45), kind=kOutput, calls=%fused_computation.6 | convolution fusion | flops 942276608 | bytes 6029316 | tf_op jit(solution)/shard_map/dot_general | solution.py:26
  87.8 9.1 %all-to-all-start.1 = ((bf16[64,8,1792]{2,1,0:T(8,128)(2,1)}), bf16[64,8,1792]{2,1,0:T(8,128)(2,1)S(1)}, u32[]{:S(2)}, u32[]{:S(2)}) async-start(bf16[64,8,1792]{2,1,0:T(8,128)(2,1)} %fusion.2), calls=%async_computation.1 | async-start | bytes 3670016 | tf_op jit(solution)/shard_map/all_to_all | solution.py:76
  97.1 1.9 %all-gather = f32[32,64]{1,0:T(8,128)S(1)} all-gather(f32[16,64]{1,0:T(8,128)S(1)} %fusion.50), channel_id=2, replica_groups=mesh['groups'=2,'ep'=64,'tp'=2] {'tp'}, dimensions={0}, use_global_device_ids=true | all-gather | bytes 12288 | tf_op jit(solution)/shard_map/all_gather | solution.py:11
  99.0 0.3 select_reduce_fusion
  99.4 0.4 fusion.51
  99.8 0.2 fusion.32
  100.0 0.2 fusion.49
  100.2 1.0 convolution_convert_fusion.2
  101.2 42.3 %all-to-all-done.1 = bf16[64,8,1792]{2,1,0:T(8,128)(2,1)S(1)} async-done(((bf16[64,8,1792]{2,1,0:T(8,128)(2,1)}), bf16[64,8,1792]{2,1,0:T(8,128)(2,1)S(1)}, u32[]{:S(2)}, u32[]{:S(2)}) %all-to-all-start.1) | async-done | bytes 1835040 | tf_op jit(solution)/shard_map/all_to_all | solution.py:76
  143.5 0.9 gather_fusion
  144.4 1.3 multiply_reduce_fusion
  (34 shorter events, 0.9 us)
Async XLA Ops:
  0.6 98.8 %copy-start = (bf16[4,256,512]{2,1,0:T(8,128)(2,1)S(1)}, bf16[4,256,512]{2,1,0:T(8,128)(2,1)}, u32[]{:S(2)}) copy-start(bf16[4,256,512]{2,1,0:T(8,128)(2,1)} %param.19) | copy-start | bytes 3145732
  69.8 3.9 %collective-permute-start = (bf16[512,1792]{1,0:T(8,128)(2,1)S(1)}, bf16[512,1792]{1,0:T(8,128)(2,1)}, u32[]{:S(2)}, u32[]{:S(2)}) collective-permute-start(bf16[512,1792]{1,0:T(8,128)(2,1)S(1)} %bitcast.58), channel_id=1, source_target_pairs={{0,1},{1,0},{2,3},{3,2},{4,5},{5,4},{6,7},{7,6},{8,9},{9,8},{10,11... | collective-permute-start | bytes 5505032 | tf_op jit(solution)/shard_map/ppermute | solution.py:16
  69.8 2.8 %copy-start.7 = (bf16[1,3584,512]{2,1,0:T(8,128)(2,1)S(1)}, bf16[1,3584,512]{2,1,0:T(8,128)(2,1)}, u32[]{:S(2)}) copy-start(bf16[1,3584,512]{2,1,0:T(8,128)(2,1)} %param.15) | copy-start | bytes 11010052
  72.6 2.0 %copy-start.6 = (bf16[1,3584,512]{2,1,0:T(8,128)(2,1)S(1)}, bf16[1,3584,512]{2,1,0:T(8,128)(2,1)}, u32[]{:S(2)}) copy-start(bf16[1,3584,512]{2,1,0:T(8,128)(2,1)} %param.14) | copy-start | bytes 11010052
  77.2 2.9 %copy-start.8 = (bf16[1,512,3584]{2,1,0:T(8,128)(2,1)S(1)}, bf16[1,512,3584]{2,1,0:T(8,128)(2,1)}, u32[]{:S(2)}) copy-start(bf16[1,512,3584]{2,1,0:T(8,128)(2,1)} %param.16) | copy-start | bytes 11010052
  81.3 4.0 %collective-permute-start.1 = (bf16[512,1792]{1,0:T(8,128)(2,1)S(1)}, bf16[512,1792]{1,0:T(8,128)(2,1)S(1)}, u32[]{:S(2)}, u32[]{:S(2)}) collective-permute-start(bf16[512,1792]{1,0:T(8,128)(2,1)S(1)} %convolution_convert_fusion), channel_id=1, source_target_pairs={{0,1},{1,0},{2,3},{3,2},{4,5},{5,4},{6,7},{7,6},{8,9},{9,8},{10,11... | collective-permute-start | bytes 5505032 | tf_op jit(solution)/shard_map/ppermute | solution.py:16
  87.7 9.2 %copy-start.1 = (bf16[1792,64]{0,1:T(8,128)(2,1)S(1)}, bf16[1792,64]{0,1:T(8,128)(2,1)}, u32[]{:S(2)}) copy-start(bf16[1792,64]{0,1:T(8,128)(2,1)} %param.13) | copy-start | bytes 688132
  87.7 9.2 %copy-start.2 = (bf16[16,1792]{1,0:T(8,128)(2,1)S(1)}, bf16[16,1792]{1,0:T(8,128)(2,1)}, u32[]{:S(2)}) copy-start(bf16[16,1792]{1,0:T(8,128)(2,1)} %param.11) | copy-start | bytes 172036
  87.7 11.6 %copy-start.9 = (s32[4]{0:T(128)S(1)}, s32[4]{0:T(128)}, u32[]{:S(2)}) copy-start(s32[4]{0:T(128)} %param.21) | copy-start | bytes 52
  87.7 11.7 %copy-start.3 = (bf16[4,32,512]{2,1,0:T(8,128)(2,1)S(1)}, bf16[4,32,512]{2,1,0:T(8,128)(2,1)}, u32[]{:S(2)}) copy-start(bf16[4,32,512]{2,1,0:T(8,128)(2,1)} %param.17) | copy-start | bytes 393220
  87.7 12.1 %copy-start.4 = (bf16[4,64,256]{2,1,0:T(8,128)(2,1)S(1)}, bf16[4,64,256]{2,1,0:T(8,128)(2,1)}, u32[]{:S(2)}) copy-start(bf16[4,64,256]{2,1,0:T(8,128)(2,1)} %param.20) | copy-start | bytes 393220
  87.7 12.1 %copy-start.5 = (bf16[4,32,64]{2,1,0:T(8,128)(2,1)S(1)}, bf16[4,32,64]{2,1,0:T(8,128)(2,1)}, u32[]{:S(2)}) copy-start(bf16[4,32,64]{2,1,0:T(8,128)(2,1)} %param.18) | copy-start | bytes 49156
  87.8 55.8 %all-to-all-start.1 = ((bf16[64,8,1792]{2,1,0:T(8,128)(2,1)}), bf16[64,8,1792]{2,1,0:T(8,128)(2,1)S(1)}, u32[]{:S(2)}, u32[]{:S(2)}) async-start(bf16[64,8,1792]{2,1,0:T(8,128)(2,1)} %fusion.2), calls=%async_computation.1 | async-start | bytes 3670016 | tf_op jit(solution)/shard_map/all_to_all | solution.py:76
